TPU v7x, 32 devices: a whole 2x2x4 slice. The times are simulated.
32 devices in a mesh: dp: 8 (over y, x, core), tp: 4 (over z).
Axes of the slice: x: 2, y: 2, z: 4, core: 2. Of those that a mesh axis runs over, the one named last changes fastest.
Arguments:
- resid: bfloat16 [2048, 4096], P('dp'), may hold values from -6 to 6
- gain: bfloat16 [4096], replicated, may hold values from 0.25 to 1.75
- grad_q: bfloat16 [2048, 3072], P('dp', 'tp'), may hold values from -1.25 to 1.25
- w_query: bfloat16 [3072, 4096], P('tp'), may hold values from -0.375 to 0.375
- grad_in: bfloat16 [2048, 4096], P('dp'), may hold values from -2 to 2
Outputs:
- weight_grad: float32 [3072, 4096], P(('tp', 'dp'))
- gain_grad: float32 [4096], replicated
- grad_out: bfloat16 [2048, 4096], P('dp')
All inputs are finite; a program needn't handle non-finite values.
Results may differ from a plain program's by a relative error of at most 0.014.
Values may be sent and summed in bfloat16 or wider, within the bound.
A program may use at most 128 MiB of HBM per device.

v0:
```python
import jax
import jax.numpy as jnp
from jax import lax
from jax.sharding import PartitionSpec as P


def norm_rows(rows_bf, gain_f):
    rows_f = rows_bf.astype(jnp.float32)
    inv_rms = lax.rsqrt(jnp.mean(rows_f * rows_f, axis=-1, keepdims=True) + 1e-05)
    unit = rows_f * inv_rms
    return (inv_rms, unit, (unit * gain_f).astype(jnp.bfloat16))


def per_device(resid, gain, grad_q, w_query, grad_in):
    gain_f = gain.astype(jnp.float32)
    inv_rms, unit, normed = norm_rows(resid, gain_f)
    local_term = jnp.dot(grad_q, w_query, preferred_element_type=jnp.float32)
    dnormed = lax.psum(local_term.astype(jnp.bfloat16), "tp").astype(jnp.float32)
    full_grad = lax.dot_general(
        grad_q, normed, (((0,), (0,)), ((), ())), preferred_element_type=jnp.float32
    )
    weight_grad = lax.psum_scatter(full_grad, "dp", scatter_dimension=0, tiled=True)
    gain_grad = lax.psum(jnp.sum(dnormed * unit, axis=0), "dp")
    dunit = dnormed * gain_f
    inner = jnp.mean(dunit * unit, axis=-1, keepdims=True)
    grad_rows = (grad_in.astype(jnp.float32) + inv_rms * (dunit - unit * inner)).astype(
        jnp.bfloat16
    )
    return (weight_grad, gain_grad, grad_rows)


def solution(mesh):
    return jax.shard_map(
        per_device,
        mesh=mesh,
        in_specs=(P("dp", None), P(), P("dp", "tp"), P("tp", None), P("dp", None)),
        out_specs=(P(("tp", "dp"), None), P(), P("dp", None)),
        check_vma=False,
    )
```

profile of v0, /device:TPU:0, one launch (start us, length us, event | category | flops | bytes accessed | tf_op | source)
XLA Modules:
  0.0 145.5 jit_solution(15786352697211024213)
XLA Ops:
  8.0 0.0 copy-start
  8.0 0.0 copy-start.2
  8.0 0.0 copy-start.1
  8.0 0.0 all-reduce.2.cloned.1.call-start
  8.1 0.9 copy-done
  9.0 5.9 %convolution_convert_fusion = bf16[256,4096]{1,0:T(8,128)(2,1)} fusion(bf16[256,768]{1,0:T(8,128)(2,1)S(1)} %copy-done, bf16[768,4096]{1,0:T(8,128)(2,1)} %param.8), kind=kOutput, calls=%fused_computation.8 | convolution fusion | flops 1611661312 | bytes 8781824 | tf_op jit(solution)/shard_map/dot_general | solution.py:17
  14.9 0.0 all-reduce.2.cloned.1.call-update
  14.9 0.0 reduce-scatter.4.cloned.1.call-start
  15.0 0.0 copy-done.2
  15.0 0.0 copy-done.1
  15.0 0.5 fusion.9
  15.5 6.6 %convolution_bitcast_fusion = f32[768,4096]{0,1:T(8,128)} fusion(bf16[256,768]{1,0:T(8,128)(2,1)S(1)} %copy-done, bf16[256,4096]{1,0:T(8,128)(2,1)S(1)} %copy-done.1, f32[4096]{0:T(1024)S(1)} %convert_element_type.22, f32[256]{0:T(256)S(1)} %add_rsqrt_fusion), kind=kOutput, calls=%fused_computation | convolution fusion | flops 1614807040 | bytes 15090688 | tf_op jit(solution)/shard_map/dot_general | solution.py:19
  22.1 12.9 %copy.10 = f32[768,4096]{1,0:T(8,128)} copy(f32[768,4096]{0,1:T(8,128)} %convolution_bitcast_fusion) | data formatting | bytes 25165824
  35.0 0.0 reduce-scatter.4.cloned.1.call-update
  35.1 68.9 %all-reduce.2.cloned.1.call-done = bf16[256,4096]{1,0:T(8,128)(2,1)} async-done(((bf16[256,4096]{1,0:T(8,128)(2,1)}), bf16[256,4096]{1,0:T(8,128)(2,1)}) %all-reduce.2.cloned.1.call-update) | async-done | bytes 2097168 | tf_op jit(solution)/shard_map/psum | solution.py:18
  103.9 3.3 %fusion.8 = (f32[256]{0:T(256)S(1)}, f32[4096]{0:T(1024)S(1)}) fusion(bf16[256,4096]{1,0:T(8,128)(2,1)S(1)} %copy-done.1, bf16[256,4096]{1,0:T(8,128)(2,1)} %all-reduce.2.cloned.1.call-done, f32[4096]{0:T(1024)S(1)} %convert_element_type.22, f32[256]{0:T(256)S(1)} %add_rsqrt_fusion), kind=kLoop, calls=%fused_computation.14 | loop fusion | flops 8384256 | bytes 4229120 | tf_op jit(solution)/shard_map/reduce_sum | solution.py:25
  107.2 25.7 %psum.15 = f32[4096]{0:T(1024)} all-reduce(f32[4096]{0:T(1024)S(1)} %get-tuple-element.10), channel_id=1, replica_groups=mesh['dp'=8,'tp'=4] {'dp'}, use_global_device_ids=true, to_apply=%region_4.0 | all-reduce | flops 4096 | bytes 32768 | tf_op jit(solution)/shard_map/psum | solution.py:23
  132.9 5.1 %fusion.6 = bf16[256,4096]{1,0:T(8,128)(2,1)} fusion(bf16[256,4096]{1,0:T(8,128)(2,1)} %all-reduce.2.cloned.1.call-done, bf16[256,4096]{1,0:T(8,128)(2,1)S(1)} %copy-done.1, bf16[256,4096]{1,0:T(8,128)(2,1)} %param.9, f32[256]{0:T(256)S(1)} %broadcast_multiply_fusion, f32[4096]{0:T(1024)S(1)} %convert_element_type.22, f32[256]{0:T(256)S(1)} %add_rsqrt_fusion), kind=kLoop, calls=%fused_computation.12 | loop fusion | flops 10485760 | bytes 8407040 | tf_op jit(solution)/shard_map/convert_element_type | solution.py:26
  138.0 0.0 reduce-scatter.4.cloned.1.call-done
  (3 shorter events, 0.0 us)
Async XLA Ops:
  8.0 1.0 copy-start
  8.0 7.0 %copy-start.2 = (bf16[4096]{0:T(1024)(128)(2,1)S(1)}, bf16[4096]{0:T(1024)(128)(2,1)}, u32[]{:S(2)}) copy-start(bf16[4096]{0:T(1024)(128)(2,1)} %param.6) | copy-start | bytes 24580
  8.0 7.0 %copy-start.1 = (bf16[256,4096]{1,0:T(8,128)(2,1)S(1)}, bf16[256,4096]{1,0:T(8,128)(2,1)}, u32[]{:S(2)}) copy-start(bf16[256,4096]{1,0:T(8,128)(2,1)} %param.5) | copy-start | bytes 6291460
  8.0 95.9 %all-reduce.2.cloned.1.call-start = ((), (), s32[]{:S(2)}) async-start(), calls=%async_computation.1 | async-start | bytes 4194304 | tf_op jit(solution)/shard_map/psum | solution.py:18
  14.9 123.1 %reduce-scatter.4.cloned.1.call-start = ((), (), s32[]{:S(2)}) async-start(), calls=%async_computation.2 | async-start | bytes 14155776
Sparse Core Ops, SparseCore 0:
  15.0 88.8 all-reduce.1
Sparse Core Ops, SparseCore 1:
  35.1 95.2 reduce-scatter.3
where the time goes:
time: 146 us; the launch traced here: 145 us
  waiting for transfers between devices  68.9 us (47%)
  blocking collectives  25.7 us (18%)
  between operations  15.5 us (11%)
  local copies, waits for them, and re-layouts  13.9 us (10%)
  matrix products  12.5 us (9%)
  other arithmetic  8.89 us (6%)
    psum x1, waiting for transfers between devices, per_device(): lax.psum(local_term.astype(jnp.bfloat16), 'tp').astype(jnp.float32)  68.9 us
    psum x1, blocking collectives, per_device(): gain_grad = lax.psum(jnp.sum(dnormed * unit, axis=0), 'dp')  25.7 us
    unnamed x7, local copies, waits for them, and re-layouts  13.9 us
    dot_general x1, matrix products, per_device(): lax.dot_general(grad_q, normed, (((0,), (0,)), ((), ())), preferred_eleme...  6.6 us
    dot_general x1, matrix products, per_device(): local_term = jnp.dot(grad_q, w_query, preferred_element_type=jnp.float32)  5.9 us
    convert_element_type x1, other arithmetic, per_device(): (grad_in.astype(jnp.float32) + inv_rms * (dunit - unit * inner)).astype(j...  5.12 us
    reduce_sum x1, other arithmetic, per_device(): inner = jnp.mean(dunit * unit, axis=-1, keepdims=True)  3.26 us
  transfers between devices with their start and end apart: 2, of which 1 were waited for; matrix products, arithmetic and copies ran while one was open for 20% of the time, Pallas kernels for 0%

commit v1 on v0

--- a/solution.py
+++ b/solution.py
@@ -1,7 +1,16 @@
+import functools
 import jax
 import jax.numpy as jnp
 from jax import lax
 from jax.sharding import PartitionSpec as P
+
+
+def streams_guide(here_x, lane_axis):
+    answer = lax.all_gather(here_x, lane_axis)
+    return jnp.sum(answer, axis=0)
+
+
+track_lanes = functools.partial(streams_guide, lane_axis="dp")
 
 
 def norm_rows(rows_bf, gain_f):
@@ -20,7 +29,7 @@
         grad_q, normed, (((0,), (0,)), ((), ())), preferred_element_type=jnp.float32
     )
     weight_grad = lax.psum_scatter(full_grad, "dp", scatter_dimension=0, tiled=True)
-    gain_grad = lax.psum(jnp.sum(dnormed * unit, axis=0), "dp")
+    gain_grad = track_lanes(jnp.sum(dnormed * unit, axis=0))
     dunit = dnormed * gain_f
     inner = jnp.mean(dunit * unit, axis=-1, keepdims=True)
     grad_rows = (grad_in.astype(jnp.float32) + inv_rms * (dunit - unit * inner)).astype(

time: 146 us -> 138 us (0.945)
  blocking collectives: 25.7 us -> 9.8 us
  waiting for transfers between devices: 68.9 us -> 76.5 us
    psum x1 -> x0, blocking collectives: 25.7 us -> none  [per_device(): gain_grad = lax.psum(jnp.sum(dnormed * unit, axis=0), 'dp')]
    all_gather x0 -> x1, blocking collectives: none -> 9.8 us  [streams_guide(): answer = lax.all_gather(here_x, lane_axis)]
    unnamed x3, waiting for transfers between devices: 0.03 us -> 7.61 us
  transfers between devices with their start and end apart: 2 -> 2, of which waited for: 1 -> 2; matrix products, arithmetic and copies ran while one was open for 20% -> 21% of each run, Pallas kernels for 0% -> 0%
where the time goes in v1:
time: 138 us
  waiting for transfers between devices  76.5 us (55%)
  between operations  15.5 us (11%)
  local copies, waits for them, and re-layouts  13.9 us (10%)
  matrix products  12.5 us (9%)
  blocking collectives  9.8 us (7%)
  other arithmetic  9.56 us (7%)
    psum x1, waiting for transfers between devices, per_device(): lax.psum(local_term.astype(jnp.bfloat16), 'tp').astype(jnp.float32)  68.9 us
    unnamed x7, local copies, waits for them, and re-layouts  13.9 us
    all_gather x1, blocking collectives, streams_guide(): answer = lax.all_gather(here_x, lane_axis)  9.8 us
    unnamed x3, waiting for transfers between devices  7.61 us
    dot_general x1, matrix products, per_device(): lax.dot_general(grad_q, normed, (((0,), (0,)), ((), ())), preferred_eleme...  6.6 us
    dot_general x1, matrix products, per_device(): local_term = jnp.dot(grad_q, w_query, preferred_element_type=jnp.float32)  5.9 us
    convert_element_type x1, other arithmetic, per_device(): (grad_in.astype(jnp.float32) + inv_rms * (dunit - unit * inner)).astype(j...  5.15 us
    reduce_sum x1, other arithmetic, per_device(): inner = jnp.mean(dunit * unit, axis=-1, keepdims=True)  3.26 us
  transfers between devices with their start and end apart: 2, of which 2 were waited for; matrix products, arithmetic and copies ran while one was open for 21% of the time, Pallas kernels for 0%

profile of v1, /device:TPU:0, one launch (start us, length us, event | category | flops | bytes accessed | tf_op | source)
XLA Modules:
  0.0 137.8 jit_solution(3946373238020914284)
XLA Ops:
  8.0 0.0 copy-start
  8.0 0.0 copy-start.2
  8.0 0.0 copy-start.1
  8.0 0.0 all-reduce.2.cloned.1.call-start
  8.1 0.9 copy-done
  9.0 5.9 %convolution_convert_fusion = bf16[256,4096]{1,0:T(8,128)(2,1)} fusion(bf16[256,768]{1,0:T(8,128)(2,1)S(1)} %copy-done, bf16[768,4096]{1,0:T(8,128)(2,1)} %param.8), kind=kOutput, calls=%fused_computation.8 | convolution fusion | flops 1611661312 | bytes 8781824 | tf_op jit(solution)/shard_map/dot_general | solution.py:26
  14.9 0.0 all-reduce.2.cloned.1.call-update
  14.9 0.0 reduce-scatter.4.cloned.1.call-start
  15.0 0.0 copy-done.2
  15.0 0.0 copy-done.1
  15.0 0.5 fusion.9
  15.5 6.6 %convolution_bitcast_fusion = f32[768,4096]{0,1:T(8,128)} fusion(bf16[256,768]{1,0:T(8,128)(2,1)S(1)} %copy-done, bf16[256,4096]{1,0:T(8,128)(2,1)S(1)} %copy-done.1, f32[4096]{0:T(1024)S(1)} %convert_element_type.22, f32[256]{0:T(256)S(1)} %add_rsqrt_fusion), kind=kOutput, calls=%fused_computation | convolution fusion | flops 1614807040 | bytes 15090688 | tf_op jit(solution)/shard_map/dot_general | solution.py:28
  22.1 12.9 %copy.11 = f32[768,4096]{1,0:T(8,128)} copy(f32[768,4096]{0,1:T(8,128)} %convolution_bitcast_fusion) | data formatting | bytes 25165824
  35.0 0.0 reduce-scatter.4.cloned.1.call-update
  35.1 68.9 %all-reduce.2.cloned.1.call-done = bf16[256,4096]{1,0:T(8,128)(2,1)} async-done(((bf16[256,4096]{1,0:T(8,128)(2,1)}), bf16[256,4096]{1,0:T(8,128)(2,1)}) %all-reduce.2.cloned.1.call-update) | async-done | bytes 2097168 | tf_op jit(solution)/shard_map/psum | solution.py:27
  103.9 3.3 %fusion.8 = (f32[256]{0:T(256)S(1)}, f32[4096]{0:T(1024)S(1)}) fusion(bf16[256,4096]{1,0:T(8,128)(2,1)S(1)} %copy-done.1, bf16[256,4096]{1,0:T(8,128)(2,1)} %all-reduce.2.cloned.1.call-done, f32[4096]{0:T(1024)S(1)} %convert_element_type.22, f32[256]{0:T(256)S(1)} %add_rsqrt_fusion), kind=kLoop, calls=%fused_computation.14 | loop fusion | flops 8384256 | bytes 4229120 | tf_op jit(solution)/shard_map/reduce_sum | solution.py:34
  107.2 9.8 %all-gather = f32[32768]{0:T(1024)S(1)} all-gather(f32[4096]{0:T(1024)S(1)} %get-tuple-element.13), channel_id=2, replica_groups=mesh['dp'=8,'tp'=4] {'dp'}, dimensions={0}, use_global_device_ids=true | all-gather | bytes 147456 | tf_op jit(solution)/shard_map/all_gather | solution.py:9
  117.0 0.6 reduce_sum.38
  117.7 5.2 %fusion.6 = bf16[256,4096]{1,0:T(8,128)(2,1)} fusion(bf16[256,4096]{1,0:T(8,128)(2,1)} %all-reduce.2.cloned.1.call-done, bf16[256,4096]{1,0:T(8,128)(2,1)S(1)} %copy-done.1, bf16[256,4096]{1,0:T(8,128)(2,1)} %param.9, f32[256]{0:T(256)S(1)} %broadcast_multiply_fusion, f32[4096]{0:T(1024)S(1)} %convert_element_type.22, f32[256]{0:T(256)S(1)} %add_rsqrt_fusion), kind=kLoop, calls=%fused_computation.12 | loop fusion | flops 10485760 | bytes 8407040 | tf_op jit(solution)/shard_map/convert_element_type | solution.py:35
  122.8 7.6 %reduce-scatter.4.cloned.1.call-done = f32[96,4096]{1,0:T(8,128)} async-done(((f32[768,4096]{1,0:T(8,128)}), f32[96,4096]{1,0:T(8,128)}) %reduce-scatter.4.cloned.1.call-update) | async-done | bytes 1572880
  (4 shorter events, 0.0 us)
Async XLA Ops:
  8.0 1.0 copy-start
  8.0 7.0 %copy-start.2 = (bf16[4096]{0:T(1024)(128)(2,1)S(1)}, bf16[4096]{0:T(1024)(128)(2,1)}, u32[]{:S(2)}) copy-start(bf16[4096]{0:T(1024)(128)(2,1)} %param.6) | copy-start | bytes 24580
  8.0 7.0 %copy-start.1 = (bf16[256,4096]{1,0:T(8,128)(2,1)S(1)}, bf16[256,4096]{1,0:T(8,128)(2,1)}, u32[]{:S(2)}) copy-start(bf16[256,4096]{1,0:T(8,128)(2,1)} %param.5) | copy-start | bytes 6291460
  8.0 95.9 %all-reduce.2.cloned.1.call-start = ((), (), s32[]{:S(2)}) async-start(), calls=%async_computation.1 | async-start | bytes 4194304 | tf_op jit(solution)/shard_map/psum | solution.py:27
  14.9 115.5 %reduce-scatter.4.cloned.1.call-start = ((), (), s32[]{:S(2)}) async-start(), calls=%async_computation.2 | async-start | bytes 14155776
Sparse Core Ops, SparseCore 0:
  15.0 88.8 all-reduce.1
Sparse Core Ops, SparseCore 1:
  35.1 95.2 reduce-scatter.3

commit v2 on v0

--- a/solution.py
+++ b/solution.py
@@ -2,6 +2,12 @@
 import jax.numpy as jnp
 from jax import lax
 from jax.sharding import PartitionSpec as P
+
+
+def summed_here(x, axis):
+    pieces = lax.all_gather(x, axis, axis=0, tiled=False)
+    total = pieces.sum(axis=0)
+    return total
 
 
 def norm_rows(rows_bf, gain_f):
@@ -15,7 +21,7 @@
     gain_f = gain.astype(jnp.float32)
     inv_rms, unit, normed = norm_rows(resid, gain_f)
     local_term = jnp.dot(grad_q, w_query, preferred_element_type=jnp.float32)
-    dnormed = lax.psum(local_term.astype(jnp.bfloat16), "tp").astype(jnp.float32)
+    dnormed = summed_here(local_term.astype(jnp.bfloat16), "tp").astype(jnp.float32)
     full_grad = lax.dot_general(
         grad_q, normed, (((0,), (0,)), ((), ())), preferred_element_type=jnp.float32
     )

time: 146 us -> 215 us (1.47)
  waiting for transfers between devices: 68.9 us -> 132 us
  other arithmetic: 8.89 us -> 15.8 us
    all_gather x0 -> x1, waiting for transfers between devices: none -> 132 us  [summed_here(): pieces = lax.all_gather(x, axis, axis=0, tiled=False)]
    psum x1 -> x0, waiting for transfers between devices: 68.9 us -> none  [per_device(): lax.psum(local_term.astype(jnp.bfloat16), 'tp').astype(jnp.float32)]
    reduce_sum x0 -> x1, other arithmetic: none -> 6.89 us  [summed_here(): total = pieces.sum(axis=0)]
  transfers between devices with their start and end apart: 2 -> 2, of which waited for: 1 -> 1; matrix products, arithmetic and copies ran while one was open for 20% -> 16% of each run, Pallas kernels for 0% -> 0%
where the time goes in v2:
time: 215 us
  waiting for transfers between devices  132 us (61%)
  blocking collectives  24.7 us (11%)
  other arithmetic  15.8 us (7%)
  between operations  15.5 us (7%)
  local copies, waits for them, and re-layouts  13.9 us (6%)
  matrix products  12.5 us (6%)
    all_gather x1, waiting for transfers between devices, summed_here(): pieces = lax.all_gather(x, axis, axis=0, tiled=False)  132 us
    psum x1, blocking collectives, per_device(): gain_grad = lax.psum(jnp.sum(dnormed * unit, axis=0), 'dp')  24.7 us
    unnamed x7, local copies, waits for them, and re-layouts  13.9 us
    reduce_sum x1, other arithmetic, summed_here(): total = pieces.sum(axis=0)  6.89 us
    dot_general x1, matrix products, per_device(): lax.dot_general(grad_q, normed, (((0,), (0,)), ((), ())), preferred_eleme...  6.58 us
    dot_general x1, matrix products, per_device(): local_term = jnp.dot(grad_q, w_query, preferred_element_type=jnp.float32)  5.9 us
    convert_element_type x1, other arithmetic, per_device(): (grad_in.astype(jnp.float32) + inv_rms * (dunit - unit * inner)).astype(j...  5.15 us
  transfers between devices with their start and end apart: 2, of which 1 were waited for; matrix products, arithmetic and copies ran while one was open for 16% of the time, Pallas kernels for 0%

profile of v2, /device:TPU:0, one launch (start us, length us, event | category | flops | bytes accessed | tf_op | source)
XLA Modules:
  0.0 214.9 jit_solution(2445045716249100223)
XLA Ops:
  8.0 0.0 copy-start
  8.0 0.0 copy-start.2
  8.0 0.0 copy-start.1
  8.0 0.0 all-gather.3.cloned.1.call-start
  8.1 0.9 copy-done
  9.0 5.9 %convolution_convert_fusion = bf16[256,4096]{1,0:T(8,128)(2,1)} fusion(bf16[256,768]{1,0:T(8,128)(2,1)S(1)} %copy-done, bf16[768,4096]{1,0:T(8,128)(2,1)} %param.8), kind=kOutput, calls=%fused_computation.8 | convolution fusion | flops 1611661312 | bytes 8781824 | tf_op jit(solution)/shard_map/dot_general | solution.py:23
  14.9 0.0 all-gather.3.cloned.1.call-update
  14.9 0.0 reduce-scatter.4.cloned.1.call-start
  15.0 0.0 copy-done.2
  15.0 0.0 copy-done.1
  15.0 0.5 fusion.9
  15.5 6.6 %convolution_bitcast_fusion = f32[768,4096]{0,1:T(8,128)} fusion(bf16[256,768]{1,0:T(8,128)(2,1)S(1)} %copy-done, bf16[256,4096]{1,0:T(8,128)(2,1)S(1)} %copy-done.1, f32[4096]{0:T(1024)S(1)} %convert_element_type.24, f32[256]{0:T(256)S(1)} %add_rsqrt_fusion), kind=kOutput, calls=%fused_computation | convolution fusion | flops 1614807040 | bytes 15090688 | tf_op jit(solution)/shard_map/dot_general | solution.py:25
  22.1 12.9 %copy.10 = f32[768,4096]{1,0:T(8,128)} copy(f32[768,4096]{0,1:T(8,128)} %convolution_bitcast_fusion) | data formatting | bytes 25165824
  35.0 0.0 reduce-scatter.4.cloned.1.call-update
  35.0 132.4 %all-gather.3.cloned.1.call-done = bf16[1024,4096]{1,0:T(8,128)(2,1)} async-done(((bf16[256,4096]{1,0:T(8,128)(2,1)}), bf16[1024,4096]{1,0:T(8,128)(2,1)}) %all-gather.3.cloned.1.call-update) | async-done | bytes 8388624 | tf_op jit(solution)/shard_map/all_gather | solution.py:8
  167.4 6.9 %reduce_sum.40 = bf16[256,4096]{1,0:T(8,128)(2,1)} reduce(bf16[4,256,4096]{2,1,0:T(8,128)(2,1)} %bitcast.7, bf16[]{:T(256)} %constant.9.clone.1), dimensions={0}, to_apply=%region_2.0 | reduce | flops 3145728 | bytes 10485762 | tf_op jit(solution)/shard_map/reduce_sum | solution.py:9
  174.3 3.3 %fusion.8 = (f32[256]{0:T(256)S(1)}, f32[4096]{0:T(1024)S(1)}) fusion(bf16[256,4096]{1,0:T(8,128)(2,1)S(1)} %copy-done.1, bf16[256,4096]{1,0:T(8,128)(2,1)} %reduce_sum.40, f32[4096]{0:T(1024)S(1)} %convert_element_type.24, f32[256]{0:T(256)S(1)} %add_rsqrt_fusion), kind=kLoop, calls=%fused_computation.14 | loop fusion | flops 8384256 | bytes 4229120 | tf_op jit(solution)/shard_map/reduce_sum | solution.py:31
  177.6 24.7 %psum.7 = f32[4096]{0:T(1024)} all-reduce(f32[4096]{0:T(1024)S(1)} %get-tuple-element.10), channel_id=1, replica_groups=mesh['dp'=8,'tp'=4] {'dp'}, use_global_device_ids=true, to_apply=%region_4.0 | all-reduce | flops 4096 | bytes 32768 | tf_op jit(solution)/shard_map/psum | solution.py:29
  202.3 5.2 %fusion.6 = bf16[256,4096]{1,0:T(8,128)(2,1)} fusion(bf16[256,4096]{1,0:T(8,128)(2,1)} %reduce_sum.40, bf16[256,4096]{1,0:T(8,128)(2,1)S(1)} %copy-done.1, bf16[256,4096]{1,0:T(8,128)(2,1)} %param.9, f32[256]{0:T(256)S(1)} %broadcast_multiply_fusion, f32[4096]{0:T(1024)S(1)} %convert_element_type.24, f32[256]{0:T(256)S(1)} %add_rsqrt_fusion), kind=kLoop, calls=%fused_computation.12 | loop fusion | flops 10485760 | bytes 8407040 | tf_op jit(solution)/shard_map/convert_element_type | solution.py:32
  207.5 0.0 reduce-scatter.4.cloned.1.call-done
  (3 shorter events, 0.0 us)
Async XLA Ops:
  8.0 1.0 copy-start
  8.0 7.0 %copy-start.2 = (bf16[4096]{0:T(1024)(128)(2,1)S(1)}, bf16[4096]{0:T(1024)(128)(2,1)}, u32[]{:S(2)}) copy-start(bf16[4096]{0:T(1024)(128)(2,1)} %param.6) | copy-start | bytes 24580
  8.0 7.0 %copy-start.1 = (bf16[256,4096]{1,0:T(8,128)(2,1)S(1)}, bf16[256,4096]{1,0:T(8,128)(2,1)}, u32[]{:S(2)}) copy-start(bf16[256,4096]{1,0:T(8,128)(2,1)} %param.5) | copy-start | bytes 6291460
  8.0 159.4 %all-gather.3.cloned.1.call-start = ((), (), s32[]{:S(2)}) async-start(), calls=%async_computation.1 | async-start | bytes 10485760 | tf_op jit(solution)/shard_map/all_gather | solution.py:8
  14.9 192.5 %reduce-scatter.4.cloned.1.call-start = ((), (), s32[]{:S(2)}) async-start(), calls=%async_computation.2 | async-start | bytes 14155776
Sparse Core Ops, SparseCore 0:
  15.0 152.3 all-gather.2
Sparse Core Ops, SparseCore 1:
  35.1 95.0 reduce-scatter.3
